TPU v7x, 256 devices: a whole 4x4x8 slice. The times are simulated.
256 devices in a mesh: dp: 8 (over y, x_hi), tok: 16 (over z, core), col: 2 (over x_lo).
Axes of the slice: x: 4 (x_hi: 2, x_lo: 2; x = x_hi * 2 + x_lo), y: 4, z: 8, core: 2. Of those that a mesh axis runs over, the one named last changes fastest.
Arguments:
- tokens: bfloat16 [8, 8192, 1024], P('dp', 'tok'), may hold values from -6 to 6
- ln_gain: bfloat16 [1024], replicated, may hold values from 0.099609375 to 1.8984375
- qkv_weight: bfloat16 [3, 1024, 512], P(None, None, 'col'), may hold values from -0.375 to 0.375
- out_weight: bfloat16 [512, 1024], P('col'), may hold values from -0.25 to 0.25
- readout_weight: bfloat16 [1024, 64], replicated, may hold values from -0.1875 to 0.1875
- conv_weight: bfloat16 [2, 64, 576], replicated, may hold values from -0.25 to 0.25
- head_weight: bfloat16 [2, 64], replicated, may hold values from -0.75 to 0.75
- holo_cot: float32 [8, 2, 32, 256], P('dp', None, 'tok', 'col'), may hold values from -1 to 1
Outputs:
- hologram: float32 [8, 2, 32, 256], P('dp', None, 'tok', 'col')
- conv_grad: float32 [2, 64, 576], replicated
- out_grad: float32 [512, 1024], P('col')
All inputs are finite; a program needn't handle non-finite values.
Results may differ from a plain program's by a relative error of at most 0.017.
The roundings to bfloat16 on the way count: a program that leaves them out, or rounds other values in their place, can miss the bound.
Values may be sent and summed in bfloat16 or wider, within the bound.
A program may use at most 128 MiB of HBM per device.

v0:
```python
import jax
import jax.numpy as jnp
from jax import lax
from jax.sharding import PartitionSpec as P

HEAD = 64
EPSILON = 1e-05


def extended(shard, sides, width):
    for axis, dim in sides:
        size, length = (lax.axis_size(axis), shard.shape[dim])
        up = [(i, (i + 1) % size) for i in range(size - 1)]
        down = [(j, i) for i, j in up]
        last = lax.slice_in_dim(shard, length - width, length, axis=dim)
        initial = lax.slice_in_dim(shard, 0, width, axis=dim)
        before = lax.ppermute(last, axis, up)
        after = lax.ppermute(initial, axis, down)
        shard = jnp.concatenate([before, shard, after], axis=dim)
    return shard


def joined_along(blocks, dim):
    shape = list(blocks.shape[1:])
    shape[dim] *= blocks.shape[0]
    return jnp.moveaxis(blocks, 0, dim).reshape(shape)


def copy_for_each(shard, axis):
    size = lax.axis_size(axis)
    return lax.all_to_all(
        jnp.broadcast_to(shard[None], (size, *shard.shape)), axis, 0, 0, tiled=True
    )


def gather_directly(shard, axis, dim):
    return joined_along(copy_for_each(shard, axis), dim)


def sent_together(arrays, axis, dim, along):
    ends, at = ([], 0)
    for a in arrays[:-1]:
        at += a.shape[along]
        ends.append(at)
    both = jnp.concatenate(arrays, axis=along)
    return tuple(jnp.split(lax.all_gather(both, axis, axis=dim, tiled=True), ends, axis=along))


def normalize(rows_in, ln_gain):
    values = rows_in.astype(jnp.float32)
    center = values - jnp.mean(values, axis=-1, keepdims=True)
    spread = jnp.mean(center * center, axis=-1, keepdims=True)
    return (center * lax.rsqrt(spread + EPSILON) * ln_gain.astype(jnp.float32)).astype(jnp.bfloat16)


def project(normed, weights_all):
    return tuple(
        (
            jnp.dot(normed, weights_all[member], preferred_element_type=jnp.float32).astype(
                jnp.bfloat16
            )
            for member in range(3)
        )
    )


def empty_state(queries):
    query_count = queries.shape[0]
    head_count = queries.shape[1] // HEAD
    return (
        jnp.zeros((query_count, head_count, HEAD), jnp.float32),
        jnp.full((head_count, query_count), -1e30, jnp.float32),
        jnp.zeros((head_count, query_count), jnp.float32),
    )


def absorb(queries, running, key_rows, value_rows):
    summed, row_top, row_total = running
    head_count = summed.shape[1]
    query_view = queries.reshape(queries.shape[0], head_count, HEAD)
    key_view = key_rows.reshape(key_rows.shape[0], head_count, HEAD)
    value_view = value_rows.reshape(value_rows.shape[0], head_count, HEAD)
    scores = jnp.einsum(
        "qhd,khd->hqk", query_view, key_view, preferred_element_type=jnp.float32
    ) * (1.0 / HEAD**0.5)
    new_top = jnp.maximum(row_top, jnp.max(scores, axis=-1))
    rescale = jnp.exp(row_top - new_top)
    raised = jnp.exp(scores - new_top[:, :, None])
    row_total = row_total * rescale + jnp.sum(raised, axis=-1)
    weighted = jnp.einsum(
        "hqk,khd->qhd", raised.astype(jnp.bfloat16), value_view, preferred_element_type=jnp.float32
    )
    summed = summed * jnp.transpose(rescale)[:, :, None] + weighted
    return (summed, new_top, row_total)


def absorb_keys(queries, running, arrived):
    key_rows, value_rows = arrived
    total_rows = key_rows.shape[0]
    block_rows = 512
    block_count = total_rows // block_rows

    def advance(turn_at, carried):
        key_block = lax.dynamic_slice_in_dim(key_rows, turn_at * block_rows, block_rows, 0)
        value_block = lax.dynamic_slice_in_dim(value_rows, turn_at * block_rows, block_rows, 0)
        return absorb(queries, carried, key_block, value_block)

    return lax.fori_loop(0, block_count, advance, running)


def finish(running):
    summed, row_top, row_total = running
    return (
        (summed / jnp.transpose(row_total)[:, :, None])
        .reshape(summed.shape[0], -1)
        .astype(jnp.bfloat16)
    )


def neighbourhood(padded, grid_rows, grid_cols):
    pieces = [
        padded[:, row_off : row_off + grid_rows, col_off : col_off + grid_cols]
        for row_off in range(3)
        for col_off in range(3)
    ]
    return jnp.concatenate(pieces, axis=0).reshape(9 * padded.shape[0], grid_rows * grid_cols)


def flipped(padded, grid_rows, grid_cols):
    pieces = [
        padded[:, 2 - row_off : 2 - row_off + grid_rows, 2 - col_off : 2 - col_off + grid_cols]
        for row_off in range(3)
        for col_off in range(3)
    ]
    return jnp.concatenate(pieces, axis=0).reshape(9 * padded.shape[0], grid_rows * grid_cols)


def transposed(weight):
    channels = weight.shape[0]
    return jnp.transpose(weight.reshape(channels, 9, channels), (2, 1, 0)).reshape(
        channels, 9 * channels
    )


def with_rims(field):
    return extended(field, (("tok", 1), ("col", 2)), 1)


def shards(
    tokens, ln_gain, qkv_weight, out_weight, readout_weight, conv_weight, head_weight, holo_cot
):
    frame_rows = tokens[0]
    cotangent = holo_cot[0]
    rows_dev = cotangent.shape[1]
    cols_dev = cotangent.shape[2]
    col_count = lax.axis_size("col")
    col_at = lax.axis_index("col")
    channels = conv_weight.shape[1]
    layer_count = conv_weight.shape[0]
    width = frame_rows.shape[1]
    own_rows = lax.dynamic_index_in_dim(
        frame_rows.reshape(rows_dev, col_count, cols_dev, width), col_at, 1, keepdims=False
    ).reshape(rows_dev * cols_dev, width)
    own_values = own_rows.astype(jnp.float32)
    readout_wide = readout_weight.astype(jnp.float32)
    readout_back = jnp.transpose(readout_wide)
    all_projections = lax.all_gather(qkv_weight, "col", axis=2, tiled=True)
    all_outputs = gather_directly(out_weight, "col", 0)
    normed = normalize(own_rows, ln_gain)
    queries, key_rows, value_rows = project(normed, all_projections)
    running = absorb_keys(
        queries, empty_state(queries), sent_together((key_rows, value_rows), ("tok", "col"), 0, 1)
    )
    context = finish(running)
    mixed = own_values + jnp.dot(context, all_outputs, preferred_element_type=jnp.float32)
    readout = jnp.dot(mixed, readout_wide, precision=lax.Precision.HIGHEST)
    hidden = jnp.transpose(readout.astype(jnp.bfloat16)).reshape(channels, rows_dev, cols_dev)
    inputs = []
    pre_acts = []
    for layer_at in range(layer_count):
        stacked = neighbourhood(with_rims(hidden), rows_dev, cols_dev)
        pre_act = jnp.dot(conv_weight[layer_at], stacked, preferred_element_type=jnp.float32)
        inputs.append(stacked)
        pre_acts.append(pre_act)
        hidden = jax.nn.silu(pre_act).astype(jnp.bfloat16).reshape(channels, rows_dev, cols_dev)
    hologram = jnp.dot(
        head_weight, hidden.reshape(channels, -1), preferred_element_type=jnp.float32
    )
    grad_hidden = jnp.dot(
        jnp.transpose(head_weight.astype(jnp.float32)),
        cotangent.reshape(cotangent.shape[0], -1),
        precision=lax.Precision.HIGHEST,
    ).astype(jnp.bfloat16)
    conv_terms = [None] * layer_count
    for layer_at in reversed(range(layer_count)):
        pre_act = pre_acts[layer_at]
        sigmoid_pre = jax.nn.sigmoid(pre_act)
        grad_pre = (
            grad_hidden.astype(jnp.float32) * sigmoid_pre * (1.0 + pre_act * (1.0 - sigmoid_pre))
        ).astype(jnp.bfloat16)
        conv_terms[layer_at] = lax.dot_general(
            grad_pre, inputs[layer_at], (((1,), (1,)), ((), ())), preferred_element_type=jnp.float32
        )
        padded = with_rims(grad_pre.reshape(channels, rows_dev, cols_dev))
        grad_hidden = jnp.dot(
            transposed(conv_weight[layer_at]),
            flipped(padded, rows_dev, cols_dev),
            preferred_element_type=jnp.float32,
        ).astype(jnp.bfloat16)
    conv_grad = lax.psum(jnp.stack(conv_terms), ("dp", "tok", "col"))
    shard_rows = out_weight.shape[0]
    small_term = lax.dot_general(
        context, grad_hidden, (((0,), (1,)), ((), ())), preferred_element_type=jnp.float32
    )
    grad_small = lax.psum(small_term, ("dp", "tok", "col"))
    own_small = lax.dynamic_slice_in_dim(grad_small, col_at * shard_rows, shard_rows, 0)
    out_grad = jnp.dot(own_small, readout_back, precision=lax.Precision.HIGHEST)
    return (hologram.reshape(1, cotangent.shape[0], rows_dev, cols_dev), conv_grad, out_grad)


def solution(mesh):
    in_specs = (
        P("dp", "tok", None),
        P(),
        P(None, None, "col"),
        P("col", None),
        P(),
        P(),
        P(),
        P("dp", None, "tok", "col"),
    )
    out_specs = (P("dp", None, "tok", "col"), P(), P("col", None))
    return jax.shard_map(shards, mesh=mesh, in_specs=in_specs, out_specs=out_specs, check_vma=False)
```

profile of v0, /device:TPU:1, one launch (start us, length us, event | category | flops | bytes accessed | tf_op | source)
XLA Modules:
  0.0 608.6 jit_solution(3435451693195484029)
XLA Ops:
  8.7 1.2 convert_reduce_fusion
  9.9 1.3 multiply_reduce_fusion
  11.2 1.3 multiply_convert_fusion
  12.6 50.8 %all-gather.3.cloned.1.call-done = bf16[3,1024,512]{2,1,0:T(8,128)(2,1)} async-done(((bf16[3,1024,256]{2,1,0:T(8,128)(2,1)}), bf16[3,1024,512]{2,1,0:T(8,128)(2,1)}) %all-gather.3.cloned.1.call-update) | async-done | bytes 3145744 | tf_op jit(solution)/shard_map/all_gather | solution.py:167
  63.4 1.7 convolution_convert_fusion.1
  65.1 1.7 convolution_convert_fusion.2
  67.7 1.1 broadcast_in_dim.28
  68.8 3.6 all-to-all-start
  72.5 1.1 dynamic-slice_convert_fusion
  73.6 1.7 convolution_convert_fusion
  75.4 107.3 %all-gather.5.cloned.1.call-done = bf16[8192,1024]{1,0:T(8,128)(2,1)} async-done(((bf16[256,1024]{1,0:T(8,128)(2,1)}), bf16[8192,1024]{1,0:T(8,128)(2,1)}) %all-gather.5.cloned.1.call-update) | async-done | bytes 16777232 | tf_op jit(solution)/shard_map/all_gather | solution.py:46
  182.7 11.3 %fusion.37 = (bf16[8192,512]{1,0:T(8,128)(2,1)}, bf16[8192,512]{1,0:T(8,128)(2,1)}) fusion(bf16[8192,1024]{1,0:T(8,128)(2,1)} %all-gather.5.cloned.1.call-done), kind=kLoop, calls=%fused_computation.157 | loop fusion | bytes 33554432 | tf_op jit(solution)/shard_map/split | solution.py:46
  194.1 67.4 %while.18 = (s32[]{:T(128)}, f32[256,8,64]{0,2,1:T(8,128)S(1)}, f32[8,256]{1,0:T(8,128)S(1)}, f32[8,256]{1,0:T(8,128)S(1)}, bf16[8192,512]{1,0:T(8,128)(2,1)}, /...) while((s32[]{:T(128)}, f32[256,8,64]{0,2,1:T(8,128)S(1)}, ...), condition=%wide.region_5.6_spmd.clone, body=%wide.region_2.5_spmd.clone.sunk | while | flops 277229568 | bytes 19267760 | solution.py:108
  194.1 1.3 constant_dynamic-slice_fusion.3
  196.6 1.0 fusion.84
  198.3 1.3 constant_dynamic-slice_fusion.3
  202.5 1.3 constant_dynamic-slice_fusion.3
  205.0 0.9 fusion.84
  206.7 1.3 constant_dynamic-slice_fusion.3
  209.2 1.0 fusion.84
  210.9 1.3 constant_dynamic-slice_fusion.3
  215.1 1.3 constant_dynamic-slice_fusion.3
  217.6 0.9 fusion.84
  219.3 1.3 constant_dynamic-slice_fusion.3
  221.9 1.0 fusion.84
  223.6 1.3 constant_dynamic-slice_fusion.3
  227.8 1.3 constant_dynamic-slice_fusion.3
  232.0 1.3 constant_dynamic-slice_fusion.3
  234.5 1.0 fusion.84
  236.2 1.3 constant_dynamic-slice_fusion.3
  240.4 1.3 constant_dynamic-slice_fusion.3
  244.6 1.3 constant_dynamic-slice_fusion.3
  247.2 1.0 fusion.84
  248.9 1.3 constant_dynamic-slice_fusion.3
  253.1 1.3 constant_dynamic-slice_fusion.3
  257.3 1.3 constant_dynamic-slice_fusion.3
  259.8 1.0 fusion.84
  261.6 1.7 convolution_add_fusion
  264.1 5.3 collective-permute-start
  269.4 1.9 collective-permute-start.1
  271.3 3.3 collective-permute-done.1
  274.8 2.0 collective-permute-start.2
  276.9 1.3 collective-permute-start.3
  278.8 3.1 collective-permute-done.3
  283.1 4.1 collective-permute-start.4
  287.2 1.9 collective-permute-start.5
  289.1 3.3 collective-permute-done.5
  292.6 1.3 collective-permute-start.6
  293.9 1.3 collective-permute-start.7
  295.9 3.1 collective-permute-done.7
  300.4 4.1 collective-permute-start.8
  304.5 1.9 collective-permute-start.9
  307.0 2.7 collective-permute-done.9
  309.9 1.3 collective-permute-start.10
  311.4 4.2 collective-permute-start.11
  317.9 3.9 collective-permute-start.12
  321.9 1.9 collective-permute-start.13
  324.0 3.3 collective-permute-done.13
  327.6 1.3 collective-permute-start.14
  329.6 4.0 collective-permute-start.15
  335.8 1.2 fusion.16
  337.7 260.2 %all-reduce.3.cloned.1.call-done = (f32[2,64,576]{2,1,0:T(8,128)}, f32[512,64]{1,0:T(8,128)}) async-done(((f32[2,64,576]{2,1,0:T(8,128)}, f32[512,64]{1,0:T(8,128)}), (f32[2,64,576]{2,1,0:T(8,128)}, f32[512,64]{1,0:T(8,128)})) %all-reduce.3.cloned.1.call-update) | async-done | bytes 426000 | tf_op jit(solution)/shard_map/psum | solution.py:210
  597.9 2.4 fusion.27
  600.3 1.7 copy.147
  (233 shorter events, 53.1 us)
Async XLA Ops:
  7.2 256.1 %copy-start = (bf16[1024,64]{0,1:T(8,128)(2,1)S(1)}, bf16[1024,64]{0,1:T(8,128)(2,1)}, u32[]{:S(2)}) copy-start(bf16[1024,64]{0,1:T(8,128)(2,1)} %param.14) | copy-start | bytes 393220
  7.2 56.2 %all-gather.3.cloned.1.call-start = ((), (), s32[]{:S(2)}) async-start(), calls=%async_computation.1 | async-start | bytes 4718592 | tf_op jit(solution)/shard_map/all_gather | solution.py:167
  7.9 59.8 %copy-start.2 = (bf16[256,1024]{1,0:T(8,128)(2,1)S(1)}, bf16[256,1024]{1,0:T(8,128)(2,1)}, u32[]{:S(2)}) copy-start(bf16[256,1024]{1,0:T(8,128)(2,1)} %param.13) | copy-start | bytes 1572868
  7.9 174.8 %all-gather.5.cloned.1.call-start = ((), (), s32[]{:S(2)}) async-start(), calls=%async_computation.2 | async-start | bytes 17301504 | tf_op jit(solution)/shard_map/all_gather | solution.py:46
  65.0 7.5 %copy-start.1 = (bf16[1,512,1024]{2,1,0:T(8,128)(2,1)S(1)}, bf16[1,512,1024]{2,1,0:T(8,128)(2,1)}, u32[]{:S(2)}) copy-start(bf16[1,512,1024]{2,1,0:T(8,128)(2,1)} %param.10) | copy-start | bytes 3145732
  68.8 192.7 %all-to-all-start = ((bf16[2,256,1024]{2,1,0:T(8,128)(2,1)}), bf16[2,256,1024]{2,1,0:T(8,128)(2,1)S(1)}, u32[]{:S(2)}, u32[]{:S(2)}) async-start(bf16[2,256,1024]{2,1,0:T(8,128)(2,1)} %broadcast_in_dim.28), calls=%async_computation | async-start | bytes 2097152 | tf_op jit(solution)/shard_map/all_to_all | solution.py:31
  72.4 525.5 %all-reduce.3.cloned.1.call-start = ((), (), s32[]{:S(2)}) async-start(), calls=%async_computation.3 | async-start | bytes 1179648 | tf_op jit(solution)/shard_map/psum | solution.py:210
  261.5 21.3 %copy-start.3 = (bf16[2,64,576]{2,1,0:T(8,128)(2,1)S(1)}, bf16[2,64,576]{2,1,0:T(8,128)(2,1)}, u32[]{:S(2)}) copy-start(bf16[2,64,576]{2,1,0:T(8,128)(2,1)} %param.15) | copy-start | bytes 442372
  261.6 38.5 %copy-start.4 = (f32[1,2,2,128]{3,2,1,0:T(2,128)S(1)}, f32[1,2,2,128]{3,2,1,0:T(2,128)}, u32[]{:S(2)}) copy-start(f32[1,2,2,128]{3,2,1,0:T(2,128)} %param.17) | copy-start | bytes 6148
  261.6 38.5 %copy-start.5 = (bf16[2,64]{1,0:T(2,128)(2,1)S(1)}, bf16[2,64]{1,0:T(2,128)(2,1)}, u32[]{:S(2)}) copy-start(bf16[2,64]{1,0:T(2,128)(2,1)} %param.16) | copy-start | bytes 772
  264.1 7.3 %collective-permute-start = (bf16[64,1,128]{2,1,0:T(2,128)(2,1)S(1)}, bf16[64,1,128]{2,1,0:T(2,128)(2,1)S(1)}, u32[]{:S(2)}, u32[]{:S(2)}) collective-permute-start(bf16[64,1,128]{2,1,0:T(2,128)(2,1)S(1)} %get-tuple-element.240), channel_id=1, source_target_pairs={{0,2},{2,4},{4,6},{6,8},{8,10},{10,12},{12,14},{14,16},{16,18},{18... | collective-permute-start | bytes 49160 | tf_op jit(solution)/shard_map/ppermute | solution.py:17
  269.4 5.2 collective-permute-start.1
  274.8 3.3 collective-permute-start.2
  276.9 5.0 collective-permute-start.3
  283.1 6.0 collective-permute-start.4
  287.2 5.2 collective-permute-start.5
  292.6 2.6 collective-permute-start.6
  293.9 5.0 collective-permute-start.7
  300.4 6.6 %collective-permute-start.8 = (bf16[64,1,128]{2,1,0:T(2,128)(2,1)S(1)}, bf16[64,1,128]{2,1,0:T(2,128)(2,1)S(1)}, u32[]{:S(2)}, u32[]{:S(2)}) collective-permute-start(bf16[64,1,128]{2,1,0:T(2,128)(2,1)S(1)} %get-tuple-element.236), channel_id=1, source_target_pairs={{0,2},{2,4},{4,6},{6,8},{8,10},{10,12},{12,14},{14,16},{16,18},{18... | collective-permute-start | bytes 49160 | tf_op jit(solution)/shard_map/ppermute | solution.py:17
  304.5 5.2 collective-permute-start.9
  309.9 5.7 collective-permute-start.10
  311.4 5.3 collective-permute-start.11
  317.9 6.1 %collective-permute-start.12 = (bf16[64,1,128]{2,1,0:T(2,128)(2,1)S(1)}, bf16[64,1,128]{2,1,0:T(2,128)(2,1)S(1)}, u32[]{:S(2)}, u32[]{:S(2)}) collective-permute-start(bf16[64,1,128]{2,1,0:T(2,128)(2,1)S(1)} %get-tuple-element.234), channel_id=1, source_target_pairs={{0,2},{2,4},{4,6},{6,8},{8,10},{10,12},{12,14},{14,16},{16,18},{18... | collective-permute-start | bytes 49160 | tf_op jit(solution)/shard_map/ppermute | solution.py:17
  321.9 5.4 collective-permute-start.13
  327.6 6.0 collective-permute-start.14
  329.6 5.3 collective-permute-start.15
Sparse Core Ops, SparseCore 0:
  9.8 53.5 all-gather.2
  67.8 114.8 all-gather.4
  337.1 260.7 all-reduce.2
where the time goes:
time: 610 us; the launch traced here: 609 us
  waiting for transfers between devices  439 us (72%)
  starting transfers between devices  45.4 us (7%)
  local copies, waits for them, and re-layouts  43.8 us (7%)
  matrix products  39.9 us (7%)
  other arithmetic  25 us (4%)
  between operations  14.5 us (2%)
    psum x1, waiting for transfers between devices, shards(): conv_grad = lax.psum(jnp.stack(conv_terms), ('dp', 'tok', 'col'))  260 us
    all_gather x1, waiting for transfers between devices, sent_together(): lax.all_gather(both, axis, axis=dim, tiled=True)  107 us
    all_gather x1, waiting for transfers between devices, shards(): all_projections = lax.all_gather(qkv_weight, 'col', axis=2, tiled=True)  50.8 us
    ppermute x8, starting transfers between devices, extended(): before = lax.ppermute(last, axis, up)  28.8 us
    dynamic_slice x32, local copies, waits for them, and re-layouts, advance(): lax.dynamic_slice_in_dim(value_rows, turn_at * block_rows, block_rows, 0)  23.8 us
    ppermute x8, waiting for transfers between devices, extended(): after = lax.ppermute(initial, axis, down)  18.7 us
    dot_general x16, matrix products, absorb(): jnp.einsum('hqk,khd->qhd', raised.astype(jnp.bfloat16), value_view, prefe...  15.2 us
    ppermute x8, starting transfers between devices, extended(): after = lax.ppermute(initial, axis, down)  12.9 us
  transfers between devices with their start and end apart: 20, of which 11 were waited for; matrix products, arithmetic and copies ran while one was open for 15% of the time, Pallas kernels for 0%

commit v1 on v0

--- a/solution.py
+++ b/solution.py
@@ -207,7 +207,7 @@
             flipped(padded, rows_dev, cols_dev),
             preferred_element_type=jnp.float32,
         ).astype(jnp.bfloat16)
-    conv_grad = lax.psum(jnp.stack(conv_terms), ("dp", "tok", "col"))
+    conv_grad = lax.psum(lax.psum(jnp.stack(conv_terms), "dp"), ("tok", "col"))
     shard_rows = out_weight.shape[0]
     small_term = lax.dot_general(
         context, grad_hidden, (((0,), (1,)), ((), ())), preferred_element_type=jnp.float32

time: 610 us -> 916 us (1.50)
  waiting for transfers between devices: 439 us -> 745 us
    psum x1 -> x3, waiting for transfers between devices: 260 us -> 566 us  [the longest x2 305 us: shards(): conv_grad = lax.psum(lax.psum(jnp.stack(conv_terms), 'dp'), ('tok', 'col'))]
  transfers between devices with their start and end apart: 20 -> 22, of which waited for: 11 -> 13; matrix products, arithmetic and copies ran while one was open for 15% -> 10% of each run, Pallas kernels for 0% -> 0%
where the time goes in v1:
time: 916 us; the launch traced here: 915 us
  waiting for transfers between devices  745 us (81%)
  starting transfers between devices  45.5 us (5%)
  local copies, waits for them, and re-layouts  43.7 us (5%)
  matrix products  39.9 us (4%)
  other arithmetic  25 us (3%)
  between operations  14.6 us (2%)
    psum x2, waiting for transfers between devices, shards(): conv_grad = lax.psum(lax.psum(jnp.stack(conv_terms), 'dp'), ('tok', 'col'))  305 us
    psum x1, waiting for transfers between devices, shards(): grad_small = lax.psum(small_term, ('dp', 'tok', 'col'))  261 us
    all_gather x1, waiting for transfers between devices, sent_together(): lax.all_gather(both, axis, axis=dim, tiled=True)  107 us
    all_gather x1, waiting for transfers between devices, shards(): all_projections = lax.all_gather(qkv_weight, 'col', axis=2, tiled=True)  50.8 us
    ppermute x8, starting transfers between devices, extended(): before = lax.ppermute(last, axis, up)  28.8 us
    dynamic_slice x32, local copies, waits for them, and re-layouts, advance(): lax.dynamic_slice_in_dim(value_rows, turn_at * block_rows, block_rows, 0)  23.8 us
    ppermute x8, waiting for transfers between devices, extended(): after = lax.ppermute(initial, axis, down)  18.7 us
  transfers between devices with their start and end apart: 22, of which 13 were waited for; matrix products, arithmetic and copies ran while one was open for 10% of the time, Pallas kernels for 0%

profile of v1, /device:TPU:1, one launch (start us, length us, event | category | flops | bytes accessed | tf_op | source)
XLA Modules:
  0.0 914.8 jit_solution(4305527492648513184)
XLA Ops:
  8.7 1.2 convert_reduce_fusion
  9.9 1.3 multiply_reduce_fusion
  11.2 1.3 multiply_convert_fusion
  12.6 50.8 %all-gather.3.cloned.1.call-done = bf16[3,1024,512]{2,1,0:T(8,128)(2,1)} async-done(((bf16[3,1024,256]{2,1,0:T(8,128)(2,1)}), bf16[3,1024,512]{2,1,0:T(8,128)(2,1)}) %all-gather.3.cloned.1.call-update) | async-done | bytes 3145744 | tf_op jit(solution)/shard_map/all_gather | solution.py:167
  63.4 1.7 convolution_convert_fusion.1
  65.1 1.7 convolution_convert_fusion.2
  67.7 1.1 broadcast_in_dim.28
  68.8 3.6 all-to-all-start
  72.5 1.1 dynamic-slice_convert_fusion
  73.6 1.7 convolution_convert_fusion
  75.4 107.3 %all-gather.5.cloned.1.call-done = bf16[8192,1024]{1,0:T(8,128)(2,1)} async-done(((bf16[256,1024]{1,0:T(8,128)(2,1)}), bf16[8192,1024]{1,0:T(8,128)(2,1)}) %all-gather.5.cloned.1.call-update) | async-done | bytes 16777232 | tf_op jit(solution)/shard_map/all_gather | solution.py:46
  182.7 11.3 %fusion.37 = (bf16[8192,512]{1,0:T(8,128)(2,1)}, bf16[8192,512]{1,0:T(8,128)(2,1)}) fusion(bf16[8192,1024]{1,0:T(8,128)(2,1)} %all-gather.5.cloned.1.call-done), kind=kLoop, calls=%fused_computation.157 | loop fusion | bytes 33554432 | tf_op jit(solution)/shard_map/split | solution.py:46
  194.0 67.4 %while.18 = (s32[]{:T(128)}, f32[256,8,64]{0,2,1:T(8,128)S(1)}, f32[8,256]{1,0:T(8,128)S(1)}, f32[8,256]{1,0:T(8,128)S(1)}, bf16[8192,512]{1,0:T(8,128)(2,1)}, /...) while((s32[]{:T(128)}, f32[256,8,64]{0,2,1:T(8,128)S(1)}, ...), condition=%wide.region_5.6_spmd.clone, body=%wide.region_2.5_spmd.clone.sunk | while | flops 277229568 | bytes 19267760 | solution.py:108
  194.0 1.3 constant_dynamic-slice_fusion.3
  196.5 1.0 fusion.84
  198.3 1.3 constant_dynamic-slice_fusion.3
  202.5 1.3 constant_dynamic-slice_fusion.3
  206.7 1.3 constant_dynamic-slice_fusion.3
  209.2 1.0 fusion.84
  210.9 1.3 constant_dynamic-slice_fusion.3
  215.1 1.3 constant_dynamic-slice_fusion.3
  219.3 1.3 constant_dynamic-slice_fusion.3
  221.8 1.0 fusion.84
  223.5 1.3 constant_dynamic-slice_fusion.3
  227.8 1.3 constant_dynamic-slice_fusion.3
  232.0 1.3 constant_dynamic-slice_fusion.3
  234.5 1.0 fusion.84
  236.2 1.3 constant_dynamic-slice_fusion.3
  240.4 1.3 constant_dynamic-slice_fusion.3
  244.6 1.3 constant_dynamic-slice_fusion.3
  247.1 1.0 fusion.84
  248.8 1.3 constant_dynamic-slice_fusion.3
  253.1 1.3 constant_dynamic-slice_fusion.3
  257.3 1.3 constant_dynamic-slice_fusion.3
  259.8 1.0 fusion.84
  261.6 1.7 convolution_add_fusion
  264.0 5.3 collective-permute-start
  269.4 1.9 collective-permute-start.1
  271.3 3.3 collective-permute-done.1
  274.8 2.0 collective-permute-start.2
  276.8 1.3 collective-permute-start.3
  278.8 3.1 collective-permute-done.3
  283.1 4.1 collective-permute-start.4
  287.1 1.9 collective-permute-start.5
  289.1 3.3 collective-permute-done.5
  292.6 1.3 collective-permute-start.6
  293.9 1.3 collective-permute-start.7
  295.9 3.1 collective-permute-done.7
  300.4 4.1 collective-permute-start.8
  304.4 1.9 collective-permute-start.9
  307.0 2.7 collective-permute-done.9
  309.9 1.3 collective-permute-start.10
  311.4 4.2 collective-permute-start.11
  317.9 3.9 collective-permute-start.12
  321.9 1.9 collective-permute-start.13
  324.0 3.3 collective-permute-done.13
  327.5 1.3 collective-permute-start.14
  329.7 4.0 collective-permute-start.15
  335.8 1.2 fusion.16
  337.1 84.5 %all-reduce.4.cloned.1.call-done = f32[2,64,576]{2,1,0:T(8,128)} async-done(((f32[2,64,576]{2,1,0:T(8,128)}), f32[2,64,576]{2,1,0:T(8,128)}) %all-reduce.4.cloned.1.call-update) | async-done | bytes 294928 | tf_op jit(solution)/shard_map/psum | solution.py:210
  422.4 260.9 %all-reduce.8.cloned.1.call-done = f32[512,64]{1,0:T(8,128)} async-done(((f32[512,64]{1,0:T(8,128)}), f32[512,64]{1,0:T(8,128)}) %all-reduce.8.cloned.1.call-update) | async-done | bytes 131088 | tf_op jit(solution)/shard_map/psum | solution.py:215
  683.3 2.4 fusion.27
  685.7 220.8 %all-reduce.6.cloned.1.call-done = f32[2,64,576]{2,1,0:T(8,128)} async-done(((f32[2,64,576]{2,1,0:T(8,128)}), f32[2,64,576]{2,1,0:T(8,128)}) %all-reduce.6.cloned.1.call-update) | async-done | bytes 294928 | tf_op jit(solution)/shard_map/psum | solution.py:210
  906.5 1.7 copy.148
  (239 shorter events, 55.2 us)
Async XLA Ops:
  7.2 256.1 %copy-start = (bf16[1024,64]{0,1:T(8,128)(2,1)S(1)}, bf16[1024,64]{0,1:T(8,128)(2,1)}, u32[]{:S(2)}) copy-start(bf16[1024,64]{0,1:T(8,128)(2,1)} %param.14) | copy-start | bytes 393220
  7.2 56.2 %all-gather.3.cloned.1.call-start = ((), (), s32[]{:S(2)}) async-start(), calls=%async_computation.1 | async-start | bytes 4718592 | tf_op jit(solution)/shard_map/all_gather | solution.py:167
  7.9 59.8 %copy-start.2 = (bf16[256,1024]{1,0:T(8,128)(2,1)S(1)}, bf16[256,1024]{1,0:T(8,128)(2,1)}, u32[]{:S(2)}) copy-start(bf16[256,1024]{1,0:T(8,128)(2,1)} %param.13) | copy-start | bytes 1572868
  7.9 174.8 %all-gather.5.cloned.1.call-start = ((), (), s32[]{:S(2)}) async-start(), calls=%async_computation.2 | async-start | bytes 17301504 | tf_op jit(solution)/shard_map/all_gather | solution.py:46
  65.0 7.4 copy-start.1
  68.8 192.7 %all-to-all-start = ((bf16[2,256,1024]{2,1,0:T(8,128)(2,1)}), bf16[2,256,1024]{2,1,0:T(8,128)(2,1)S(1)}, u32[]{:S(2)}, u32[]{:S(2)}) async-start(bf16[2,256,1024]{2,1,0:T(8,128)(2,1)} %broadcast_in_dim.28), calls=%async_computation | async-start | bytes 2097152 | tf_op jit(solution)/shard_map/all_to_all | solution.py:31
  72.4 349.2 %all-reduce.4.cloned.1.call-start = ((), (), s32[]{:S(2)}) async-start(), calls=%async_computation.3 | async-start | bytes 655360 | tf_op jit(solution)/shard_map/psum | solution.py:210
  261.5 21.3 %copy-start.3 = (bf16[2,64,576]{2,1,0:T(8,128)(2,1)S(1)}, bf16[2,64,576]{2,1,0:T(8,128)(2,1)}, u32[]{:S(2)}) copy-start(bf16[2,64,576]{2,1,0:T(8,128)(2,1)} %param.15) | copy-start | bytes 442372
  261.6 38.5 %copy-start.4 = (f32[1,2,2,128]{3,2,1,0:T(2,128)S(1)}, f32[1,2,2,128]{3,2,1,0:T(2,128)}, u32[]{:S(2)}) copy-start(f32[1,2,2,128]{3,2,1,0:T(2,128)} %param.17) | copy-start | bytes 6148
  261.6 38.5 %copy-start.5 = (bf16[2,64]{1,0:T(2,128)(2,1)S(1)}, bf16[2,64]{1,0:T(2,128)(2,1)}, u32[]{:S(2)}) copy-start(bf16[2,64]{1,0:T(2,128)(2,1)} %param.16) | copy-start | bytes 772
  264.0 7.3 collective-permute-start
  269.4 5.2 collective-permute-start.1
  274.8 3.3 collective-permute-start.2
  276.8 5.0 collective-permute-start.3
  283.1 6.0 collective-permute-start.4
  287.1 5.2 collective-permute-start.5
  292.6 2.6 collective-permute-start.6
  293.9 5.0 collective-permute-start.7
  300.4 6.6 collective-permute-start.8
  304.4 5.2 collective-permute-start.9
  309.9 5.7 collective-permute-start.10
  311.4 5.3 collective-permute-start.11
  317.9 6.1 collective-permute-start.12
  321.9 5.4 collective-permute-start.13
  327.5 6.1 collective-permute-start.14
  329.6 353.7 %all-reduce.8.cloned.1.call-start = ((), (), s32[]{:S(2)}) async-start(), calls=%async_computation.5 | async-start | bytes 524288 | tf_op jit(solution)/shard_map/psum | solution.py:215
  329.7 5.3 collective-permute-start.15
  337.1 569.5 %all-reduce.6.cloned.1.call-start = ((), (), s32[]{:S(2)}) async-start(), calls=%async_computation.4 | async-start | bytes 655360 | tf_op jit(solution)/shard_map/psum | solution.py:210
Sparse Core Ops, SparseCore 0:
  9.8 53.5 all-gather.2
  67.8 114.8 all-gather.4
  329.7 91.8 all-reduce.3
  427.5 255.7 all-reduce.7
  685.8 220.7 all-reduce.5
